TPU v7x, 16 devices: a 4x2x1 block of a 4x4x8 slice. The times are simulated.
16 devices in a mesh: data: 2 (over y, z), seq: 8 (over x, core).
Axes of the slice: x: 4, y: 2, z: 1, core: 2. Of those that a mesh axis runs over, the one named last changes fastest.
The devices are a block of a 4x4x8 slice.
Arguments:
- x: bfloat16 [64, 4096, 512], P('data', 'seq'), parts along dimension 0
- w_tok1: bfloat16 [2, 4096, 256], replicated
- b_tok1: float32 [2, 256], replicated
- w_tok2: bfloat16 [2, 256, 4096], replicated
- b_tok2: float32 [2, 4096], replicated
- w_ch1: bfloat16 [2, 512, 2048], replicated
- b_ch1: float32 [2, 2048], replicated
- w_ch2: bfloat16 [2, 2048, 512], replicated
- b_ch2: float32 [2, 512], replicated
- ln_params: float32 [2, 4, 512], replicated
Outputs:
- output: bfloat16 [64, 4096, 512], P('data', 'seq'), parts along dimension 0
There are 2 independent parts. A program takes and returns all parts, laid end to end along the dimension named above; an argument that names none is the same for every part.
All inputs are finite; a program needn't handle non-finite values.
Results may differ from a plain program's by a relative error of at most 0.0171184.
Values are sent between devices in bfloat16 or wider.
A program may use at most 768 MiB of HBM per device.

v0:
```python
import jax
import jax.numpy as jnp
from jax import lax
from jax.sharding import PartitionSpec as P

LN_EPS = 1e-6


def layer_norm(rows_in, ln_scale, ln_offset):
    row_vals = rows_in.astype(jnp.float32)
    row_mean = jnp.mean(row_vals, axis=-1, keepdims=True)
    centered = row_vals - row_mean
    row_var = jnp.mean(centered * centered, axis=-1, keepdims=True)
    return (centered * lax.rsqrt(row_var + LN_EPS) * ln_scale + ln_offset).astype(jnp.bfloat16)


def channel_block(act_in, t_tok, w_in, b_in, w_out, b_out, ln_layer):
    x_mid = (act_in.astype(jnp.float32) + t_tok.astype(jnp.float32)).astype(jnp.bfloat16)
    v_norm = layer_norm(x_mid, ln_layer[2], ln_layer[3])
    pre_act = jnp.einsum("bsc,ce->bse", v_norm, w_in, preferred_element_type=jnp.float32) + b_in
    a_act = jax.nn.gelu(pre_act, approximate=True).astype(jnp.bfloat16)
    ch_out = jnp.einsum("bse,ec->bsc", a_act, w_out, preferred_element_type=jnp.float32) + b_out
    return (x_mid.astype(jnp.float32) + ch_out).astype(jnp.bfloat16)


def solution(mesh):
    def local_layers(x_blk, w_tok1, b_tok1, w_tok2, b_tok2, w_ch1, b_ch1, w_ch2, b_ch2, ln_params):
        act_cur = x_blk
        for layer_idx in range(w_tok1.shape[0]):
            ln_layer = ln_params[layer_idx]
            u_norm = layer_norm(act_cur, ln_layer[0], ln_layer[1])
            u_cols = lax.all_to_all(u_norm, "seq", split_axis=2, concat_axis=1, tiled=True)
            hidden = jnp.einsum("sd,bsc->bdc", w_tok1[layer_idx], u_cols, preferred_element_type=jnp.float32)
            g_act = jax.nn.gelu(hidden + b_tok1[layer_idx][None, :, None], approximate=True).astype(jnp.bfloat16)
            t_sum = jnp.einsum("ds,bdc->bsc", w_tok2[layer_idx], g_act, preferred_element_type=jnp.float32)
            t_cols = (t_sum + b_tok2[layer_idx][None, :, None]).astype(jnp.bfloat16)
            t_rows = lax.all_to_all(t_cols, "seq", split_axis=1, concat_axis=2, tiled=True)
            act_cur = channel_block(act_cur, t_rows, w_ch1[layer_idx], b_ch1[layer_idx], w_ch2[layer_idx], b_ch2[layer_idx], ln_layer)
        return act_cur

    act_spec = P("data", "seq", None)
    rep_spec = P()
    return jax.shard_map(local_layers, mesh=mesh, in_specs=(act_spec,) + (rep_spec,) * 9, out_specs=act_spec, check_vma=False)
```

profile of v0, /device:TPU:112, one launch (start us, length us, event | category | flops | bytes accessed | tf_op | source)
XLA Modules:
  0.0 1582.7 jit_solution(9429132737853278201)
XLA Ops:
  0.0 22.5 %copy.21 = bf16[32,512,512]{1,2,0:T(8,128)(2,1)} copy(bf16[32,512,512]{2,1,0:T(8,128)(2,1)} %param.10) | data formatting | bytes 33554432 | tf_op args[0]
  22.5 8.4 convert_reduce_fusion.3
  30.9 2.3 copy-done
  33.1 4.6 fusion.40
  37.8 0.0 copy-done.5
  37.8 0.6 fusion.139
  38.4 7.5 fusion.43
  45.9 26.6 %copy.22 = bf16[32,512,512]{1,0,2:T(8,128)(2,1)} copy(bf16[32,512,512]{1,2,0:T(8,128)(2,1)S(1)} %fusion.43) | data formatting | bytes 33554432 | tf_op jit(solution)/shard_map/convert_element_type | solution.py:14
  72.4 6.2 all-to-all-start
  78.7 0.0 copy-done.16
  78.7 0.5 fusion.142
  79.2 0.0 copy-done.4
  79.2 0.6 fusion.138
  79.8 183.3 %all-to-all-done = bf16[32,512,512]{1,0,2:T(8,128)(2,1)} async-done(((bf16[32,512,512]{1,0,2:T(8,128)(2,1)}), bf16[32,512,512]{1,0,2:T(8,128)(2,1)}, u32[]{:S(2)}, u32[]{:S(2)}) %all-to-all-start) | async-done | bytes 16777248 | tf_op jit(solution)/shard_map/all_to_all | solution.py:32
  263.2 18.6 %copy.42 = bf16[32,512,8,64]{1,2,3,0:T(8,128)(2,1)} copy(bf16[32,512,8,64]{1,0,3,2:T(8,128)(2,1)} %bitcast.2) | data formatting | bytes 33554432 | tf_op jit(solution)/shard_map/all_to_all | solution.py:32
  281.8 25.6 %all_to_all.43 = bf16[32,4096,64]{1,2,0:T(8,128)(2,1)} reshape(bf16[32,8,512,64]{2,1,3,0:T(8,128)(2,1)} %bitcast.125) | data formatting | bytes 33554432 | tf_op jit(solution)/shard_map/all_to_all | solution.py:32
  307.4 11.6 fusion.93
  319.0 9.7 fusion.48
  328.7 45.9 %copy.24 = bf16[32,4096,64]{2,0,1:T(8,128)(2,1)} copy(bf16[32,4096,64]{1,2,0:T(8,128)(2,1)} %fusion.48) | data formatting | bytes 33554432 | tf_op jit(solution)/shard_map/convert_element_type | solution.py:36
  374.6 29.9 %reshape.92 = bf16[8,2,524288]{2,1,0:T(2,128)(2,1)} reshape(bf16[4096,32,64]{2,1,0:T(8,128)(2,1)} %bitcast.121) | data formatting | bytes 33554432
  404.4 6.1 all-to-all-start.1
  410.5 0.0 copy-done.11
  410.5 0.6 fusion.141
  411.1 0.0 copy-done.6
  411.1 0.6 fusion.140
  411.7 1.7 fusion.102.clone.5
  413.4 181.3 %all-to-all-done.1 = bf16[8,2,524288]{2,1,0:T(2,128)(2,1)} async-done(((bf16[8,2,524288]{2,1,0:T(2,128)(2,1)}), bf16[8,2,524288]{2,1,0:T(2,128)(2,1)}, u32[]{:S(2)}, u32[]{:S(2)}) %all-to-all-start.1) | async-done | bytes 16777248 | tf_op jit(solution)/shard_map/all_to_all | solution.py:37
  594.7 28.4 %reshape.93 = bf16[4096,32,64]{2,1,0:T(8,128)(2,1)} reshape(bf16[8,2,524288]{2,1,0:T(2,128)(2,1)} %all-to-all-done.1) | data formatting | bytes 33554432
  623.1 39.8 %copy.25 = f32[32,8,512,64]{2,3,1,0:T(8,128)} copy(bf16[32,8,512,64]{3,0,2,1:T(8,128)(2,1)} %bitcast.123) | data formatting | bytes 50331648 | tf_op jit(solution)/shard_map/convert_element_type | solution.py:18
  663.0 16.9 %convert_reduce_fusion.2 = (f32[32,512]{1,0:T(8,128)S(1)}, bf16[32,512,512]{1,2,0:T(8,128)(2,1)S(1)}) fusion(f32[32,8,512,64]{2,3,1,0:T(8,128)} %copy.25, bf16[32,512,512]{1,2,0:T(8,128)(2,1)} %copy.21), kind=kLoop, calls=%fused_computation.28 | loop fusion | flops 41926656 | bytes 67174400 | tf_op jit(solution)/shard_map/reduce_sum | solution.py:11
  679.9 0.0 copy-start.3
  679.9 0.0 copy-start.14
  679.9 0.0 copy-start.15
  679.9 6.1 copy-done.3
  686.0 4.6 fusion.36
  690.7 0.0 copy-done.14
  690.7 0.0 copy-done.15
  690.7 105.1 %convert_reduce_fusion.1 = (f32[32,512]{1,0:T(8,128)S(1)}, bf16[32,512,512]{1,2,0:T(8,128)(2,1)}) fusion(f32[512]{0:T(512)S(1)} %bitcast.141, f32[2048]{0:T(1024)S(1)} %bitcast.135, bf16[32,512,512]{1,2,0:T(8,128)(2,1)} %copy-done.3, f32[512]{0:T(512)S(1)} %bitcast.138, f32[512]{0:T(512)S(1)} %bitcast.139, f32[32,512]{1,0:T(8,128)S(1)} %add_rsqrt_fusion.2, ...), kind=kOutput, calls=%fused_computation.25 | convolution fusion | flops 69155667968 | bytes 54736896 | tf_op jit(solution)/shard_map/bse,ec->bsc/dot_general | solution.py:22
  795.8 0.0 copy-start.1
  795.8 0.0 copy-start.8
  795.8 0.0 copy-start.9
  795.9 9.1 fusion.32
  805.0 1.5 copy-done.1
  806.5 0.0 copy-done.9
  806.5 7.5 fusion.35
  814.0 24.7 %copy.28 = bf16[32,512,512]{1,0,2:T(8,128)(2,1)S(1)} copy(bf16[32,512,512]{1,2,0:T(8,128)(2,1)S(1)} %fusion.35) | data formatting | bytes 33554432 | tf_op jit(solution)/shard_map/convert_element_type | solution.py:14
  838.7 187.4 %all_to_all.54 = bf16[32,512,512]{1,0,2:T(8,128)(2,1)S(1)} all-to-all(bf16[32,512,512]{1,0,2:T(8,128)(2,1)S(1)} %copy.28), channel_id=1, replica_groups=mesh['data'=2,'seq'=8] {'seq'}, dimensions={2} | all-to-all | bytes 33554432 | tf_op jit(solution)/shard_map/all_to_all | solution.py:32
  1026.1 20.6 %copy.41 = bf16[32,512,8,64]{1,2,3,0:T(8,128)(2,1)} copy(bf16[32,512,8,64]{1,0,3,2:T(8,128)(2,1)S(1)} %bitcast.126) | data formatting | bytes 33554432 | tf_op jit(solution)/shard_map/all_to_all | solution.py:32
  1046.7 25.6 %all_to_all.48 = bf16[32,4096,64]{1,2,0:T(8,128)(2,1)} reshape(bf16[32,8,512,64]{2,1,3,0:T(8,128)(2,1)} %bitcast.127) | data formatting | bytes 33554432 | tf_op jit(solution)/shard_map/all_to_all | solution.py:32
  1072.3 11.6 fusion.101
  1084.0 10.1 fusion.49
  1094.1 45.9 %copy.30 = bf16[32,4096,64]{2,0,1:T(8,128)(2,1)} copy(bf16[32,4096,64]{1,2,0:T(8,128)(2,1)} %fusion.49) | data formatting | bytes 33554432 | tf_op jit(solution)/shard_map/convert_element_type | solution.py:36
  1140.0 29.8 %reshape.94 = bf16[8,2,524288]{2,1,0:T(2,128)(2,1)} reshape(bf16[4096,32,64]{2,1,0:T(8,128)(2,1)} %bitcast.122) | data formatting | bytes 33554432
  1169.8 5.9 all-to-all-start.3
  1175.8 1.7 fusion.170
  1177.5 182.5 %all-to-all-done.3 = bf16[8,2,524288]{2,1,0:T(2,128)(2,1)} async-done(((bf16[8,2,524288]{2,1,0:T(2,128)(2,1)}), bf16[8,2,524288]{2,1,0:T(2,128)(2,1)}, u32[]{:S(2)}, u32[]{:S(2)}) %all-to-all-start.3) | async-done | bytes 16777248 | tf_op jit(solution)/shard_map/all_to_all | solution.py:37
  1360.0 28.4 %reshape.95 = bf16[4096,32,64]{2,1,0:T(8,128)(2,1)} reshape(bf16[8,2,524288]{2,1,0:T(2,128)(2,1)} %all-to-all-done.3) | data formatting | bytes 33554432
  1388.4 39.8 %copy.31 = f32[32,8,512,64]{2,3,1,0:T(8,128)} copy(bf16[32,8,512,64]{3,0,2,1:T(8,128)(2,1)} %bitcast.124) | data formatting | bytes 50331648 | tf_op jit(solution)/shard_map/convert_element_type | solution.py:18
  1428.2 16.9 %convert_reduce_fusion = (f32[32,512]{1,0:T(8,128)S(1)}, bf16[32,512,512]{1,2,0:T(8,128)(2,1)S(1)}) fusion(f32[32,8,512,64]{2,3,1,0:T(8,128)} %copy.31, bf16[32,512,512]{1,2,0:T(8,128)(2,1)} %get-tuple-element.26), kind=kLoop, calls=%fused_computation.22 | loop fusion | flops 41926656 | bytes 67174400 | tf_op jit(solution)/shard_map/reduce_sum | solution.py:11
  1445.1 0.0 copy-start.2
  1445.2 6.1 copy-done.2
  1451.3 4.6 fusion.28
  1456.0 103.9 %fusion.47 = bf16[32,512,512]{1,2,0:T(8,128)(2,1)} fusion(bf16[32,512,512]{1,2,0:T(8,128)(2,1)} %copy-done.2, f32[512]{0:T(512)S(1)} %bitcast.140, f32[2048]{0:T(1024)S(1)} %bitcast.134, f32[512]{0:T(512)S(1)} %bitcast.137, f32[512]{0:T(512)S(1)} %bitcast.136, f32[32,512]{1,0:T(8,128)S(1)} %add_rsqrt_fusion, f32[32,512]{1,0:T(8,128)S(1)} %broadcast_multiply_fusion, ...), kind=kOutput, calls=%fused_computation.59 | convolution fusion | flops 69138907136 | bytes 54671360 | tf_op jit(solution)/shard_map/bse,ec->bsc/dot_general | solution.py:22
  1559.8 22.5 %copy.34 = bf16[32,512,512]{2,1,0:T(8,128)(2,1)} copy(bf16[32,512,512]{1,2,0:T(8,128)(2,1)} %fusion.47) | data formatting | bytes 33554432 | tf_op jit(solution)/shard_map/convert_element_type | solution.py:23
  (27 shorter events, 0.1 us)
Async XLA Ops:
  22.5 10.7 copy-start
  22.5 15.3 copy-start.5
  72.4 6.2 copy-start.16
  72.4 6.8 copy-start.4
  72.4 190.7 %all-to-all-start = ((bf16[32,512,512]{1,0,2:T(8,128)(2,1)}), bf16[32,512,512]{1,0,2:T(8,128)(2,1)}, u32[]{:S(2)}, u32[]{:S(2)}) async-start(bf16[32,512,512]{1,0,2:T(8,128)(2,1)} %copy.22), calls=%async_computation | async-start | bytes 33554432 | tf_op jit(solution)/shard_map/all_to_all | solution.py:32
  404.4 6.1 copy-start.11
  404.4 6.7 copy-start.6
  404.4 190.3 %all-to-all-start.1 = ((bf16[8,2,524288]{2,1,0:T(2,128)(2,1)}), bf16[8,2,524288]{2,1,0:T(2,128)(2,1)}, u32[]{:S(2)}, u32[]{:S(2)}) async-start(bf16[8,2,524288]{2,1,0:T(2,128)(2,1)} %reshape.92), calls=%async_computation.1 | async-start | bytes 33554432 | tf_op jit(solution)/shard_map/all_to_all | solution.py:37
  679.9 6.2 copy-start.3
  679.9 10.8 copy-start.14
  679.9 10.8 copy-start.15
  795.8 10.7 copy-start.1
  795.8 10.7 copy-start.8
  795.8 10.7 copy-start.9
  1046.7 25.6 %copy-start.18 = (f32[1,256]{1,0:T(1,128)S(1)}, f32[1,256]{1,0:T(1,128)}, u32[]{:S(2)}) copy-start(f32[1,256]{1,0:T(1,128)} %get-tuple-element.23) | copy-start | bytes 3076
  1072.3 11.6 copy-start.7
  1169.8 190.2 %all-to-all-start.3 = ((bf16[8,2,524288]{2,1,0:T(2,128)(2,1)}), bf16[8,2,524288]{2,1,0:T(2,128)(2,1)}, u32[]{:S(2)}, u32[]{:S(2)}) async-start(bf16[8,2,524288]{2,1,0:T(2,128)(2,1)} %reshape.94), calls=%async_computation.3 | async-start | bytes 33554432 | tf_op jit(solution)/shard_map/all_to_all | solution.py:37
  1445.1 6.2 copy-start.2
  1445.1 10.8 copy-start.10
  1445.1 10.8 copy-start.12
  1445.2 10.8 copy-start.13
  1445.2 10.8 copy-start.17
where the time goes:
time: 1600 us; the launch traced here: 1580 us
  waiting for transfers between devices  547 us (34%)
  local copies, waits for them, and re-layouts  497 us (31%)
  matrix products  252 us (16%)
  blocking collectives  187 us (12%)
  other arithmetic  80.1 us (5%)
  starting transfers between devices  18.2 us (1%)
    all_to_all x2, waiting for transfers between devices, local_layers(): lax.all_to_all(t_cols, 'seq', split_axis=1, concat_axis=2, tiled=True)  364 us
    dot_general x2, matrix products, channel_block(): jnp.einsum('bse,ec->bsc', a_act, w_out, preferred_element_type=jnp.float32)  209 us
    all_to_all x1, blocking collectives, local_layers(): lax.all_to_all(u_norm, 'seq', split_axis=2, concat_axis=1, tiled=True)  187 us
    all_to_all x1, waiting for transfers between devices, local_layers(): lax.all_to_all(u_norm, 'seq', split_axis=2, concat_axis=1, tiled=True)  183 us
    unnamed x43, local copies, waits for them, and re-layouts  155 us
    convert_element_type x2, local copies, waits for them, and re-layouts, local_layers(): t_cols = (t_sum + b_tok2[layer_idx][None, :, None]).astype(jnp.bfloat16)  91.7 us
    all_to_all x4, local copies, waits for them, and re-layouts, local_layers(): lax.all_to_all(u_norm, 'seq', split_axis=2, concat_axis=1, tiled=True)  90.4 us
    convert_element_type x2, local copies, waits for them, and re-layouts, channel_block(): t_tok.astype(jnp.float32)  79.7 us
  transfers between devices with their start and end apart: 3, of which 3 were waited for; matrix products, arithmetic and copies ran while one was open for 0% of the time, Pallas kernels for 0%

commit v1 on v0

v1 whole, which is shorter than its diff:
```python
import functools

import jax
import jax.numpy as jnp
from jax import lax
from jax.experimental import pallas as pl
from jax.experimental.pallas import tpu as pltpu
from jax.sharding import PartitionSpec as P

LN_EPS = 1e-6
CHUNKS = 4
GELU_A = 0.7978845608028654
GELU_B = 0.7978845608028654 * 0.044715


def gelu(h):
    return 0.5 * h * (1.0 + jnp.tanh(h * (GELU_A + GELU_B * (h * h))))


def norm(rows, scale, offset):
    mean = jnp.mean(rows, axis=-1, keepdims=True)
    centered = rows - mean
    var = jnp.mean(centered * centered, axis=-1, keepdims=True)
    return (centered * lax.rsqrt(var + LN_EPS) * scale + offset).astype(jnp.bfloat16)


def contract0(a, b):
    return lax.dot_general(a, b, (((0,), (0,)), ((), ())), preferred_element_type=jnp.float32)


def token_in(x, w1_ref, ln_ref):
    u = norm(x.astype(jnp.float32), ln_ref[0:1, :], ln_ref[1:2, :])
    return contract0(w1_ref[...], u)


def first_kernel(x_ref, w1_ref, ln_ref, h_ref):
    h_ref[0] = token_in(x_ref[0], w1_ref, ln_ref)


def channel(x_ref, g_ref, w2_ref, b2_ref, wc1_ref, bc1_ref, wc2_ref, bc2_ref, ln_ref, a_ref):
    t = (contract0(w2_ref[...], g_ref[0]) + b2_ref[...]).astype(jnp.bfloat16)
    x1 = (x_ref[0].astype(jnp.float32) + t.astype(jnp.float32)).astype(jnp.bfloat16)
    v = norm(x1.astype(jnp.float32), ln_ref[2:3, :], ln_ref[3:4, :])
    width = 512
    for e in range(0, wc1_ref.shape[1], width):
        cols = slice(e, e + width)
        pre = jnp.dot(v, wc1_ref[:, cols], preferred_element_type=jnp.float32) + bc1_ref[:, cols]
        a_ref[:, cols] = gelu(pre).astype(jnp.bfloat16)
    out = jnp.dot(a_ref[...], wc2_ref[...], preferred_element_type=jnp.float32) + bc2_ref[...]
    return (x1.astype(jnp.float32) + out).astype(jnp.bfloat16)


def last_kernel(x_ref, g_ref, w2_ref, b2_ref, wc1_ref, bc1_ref, wc2_ref, bc2_ref, ln_ref, z_ref, a_ref):
    z_ref[0] = channel(x_ref, g_ref, w2_ref, b2_ref, wc1_ref, bc1_ref, wc2_ref, bc2_ref, ln_ref, a_ref)


def middle_kernel(x_ref, g_ref, w2_ref, b2_ref, wc1_ref, bc1_ref, wc2_ref, bc2_ref, ln_ref, w1n_ref, lnn_ref, z_ref, h_ref, a_ref):
    z = channel(x_ref, g_ref, w2_ref, b2_ref, wc1_ref, bc1_ref, wc2_ref, bc2_ref, ln_ref, a_ref)
    z_ref[0] = z
    h_ref[0] = token_in(z, w1n_ref, lnn_ref)


def whole(a):
    return pl.BlockSpec(a.shape, lambda i: (0,) * a.ndim)


def image(shape):
    return pl.BlockSpec((1,) + shape, lambda i: (i, 0, 0))


def solution(mesh):
    def local_layers(x, w_tok1, b_tok1, w_tok2, b_tok2, w_ch1, b_ch1, w_ch2, b_ch2, ln_params):
        layers = w_tok1.shape[0]
        batch, rows, chans = x.shape
        hid = w_tok1.shape[2]
        me = lax.axis_index("seq")
        size = batch // CHUNKS
        w1 = lax.dynamic_slice_in_dim(w_tok1, me * rows, rows, 1)
        w2 = lax.dynamic_slice_in_dim(w_tok2, me * rows, rows, 2)
        b2 = lax.dynamic_slice_in_dim(b_tok2, me * rows, rows, 1)[:, :, None]
        own = hid // mesh.shape["seq"]
        b1 = lax.dynamic_slice_in_dim(b_tok1, me * own, own, 1)[:, None, :, None]
        params = pltpu.CompilerParams(vmem_limit_bytes=50 * 1024 * 1024)

        def first(xc):
            return pl.pallas_call(
                first_kernel,
                grid=(size,),
                out_shape=jax.ShapeDtypeStruct((size, hid, chans), jnp.float32),
                in_specs=[image((rows, chans)), whole(w1[0]), whole(ln_params[0])],
                out_specs=image((hid, chans)),
                compiler_params=params,
                cost_estimate=pl.CostEstimate(flops=2 * size * rows * hid * chans, bytes_accessed=size * chans * (2 * rows + 4 * hid), transcendentals=0),
            )(xc, w1[0], ln_params[0])

        def rest(l, xc, g):
            args = [xc, g, w2[l], b2[l], w_ch1[l], b_ch1[l][None], w_ch2[l], b_ch2[l][None], ln_params[l]]
            specs = [image((rows, chans)), image((hid, chans))] + [whole(a) for a in args[2:]]
            outs = [jax.ShapeDtypeStruct((size, rows, chans), jnp.bfloat16)]
            out_specs = [image((rows, chans))]
            body = last_kernel
            if l + 1 < layers:
                body = middle_kernel
                args += [w1[l + 1], ln_params[l + 1]]
                specs += [whole(a) for a in args[-2:]]
                outs.append(jax.ShapeDtypeStruct((size, hid, chans), jnp.float32))
                out_specs.append(image((hid, chans)))
            wide = w_ch1.shape[2]
            return pl.pallas_call(
                body,
                grid=(size,),
                out_shape=outs,
                in_specs=specs,
                out_specs=out_specs,
                scratch_shapes=[pltpu.VMEM((rows, wide), jnp.bfloat16)],
                compiler_params=params,
                cost_estimate=pl.CostEstimate(flops=4 * size * rows * wide * chans, bytes_accessed=4 * size * chans * rows, transcendentals=0),
            )(*args)

        xs = [x[c * size:(c + 1) * size] for c in range(CHUNKS)]
        hs = [first(xc) for xc in xs]
        for l in range(layers):
            gs = []
            for h in hs:
                part = lax.psum_scatter(h, "seq", scatter_dimension=1, tiled=True)
                g = jax.nn.gelu(part + b1[l], approximate=True).astype(jnp.bfloat16)
                gs.append(lax.all_gather(g, "seq", axis=1, tiled=True))
            res = [rest(l, xc, g) for xc, g in zip(xs, gs)]
            xs = [r[0] for r in res]
            hs = [r[1] for r in res if len(r) > 1]
        return jnp.concatenate(xs, 0)

    act = P("data", "seq", None)
    rep = P()
    return jax.shard_map(local_layers, mesh=mesh, in_specs=(act,) + (rep,) * 9, out_specs=act, check_vma=False)
```

time: 1600 us -> 584 us (0.36)
  local copies, waits for them, and re-layouts: 497 us -> 36.2 us
  waiting for transfers between devices: 547 us -> 206 us
  Pallas kernels: 0 us -> 304 us
  matrix products: 252 us -> 0 us
  blocking collectives: 187 us -> 0 us
  other arithmetic: 80.1 us -> 20.5 us
  starting transfers between devices: 18.2 us -> 1.36 us
    all_to_all x3 -> x0, waiting for transfers between devices: 547 us -> none  [the longest x2 364 us: local_layers(): lax.all_to_all(t_cols, 'seq', split_axis=1, concat_axis=2, tiled=True)]
    pallas_call x0 -> x12, Pallas kernels: none -> 304 us  [the longest x8 268 us: rest(): pl.pallas_call(body, grid=(size,), out_shape=outs, in_specs=specs, out_sp...]
    dot_general x6 -> x0, matrix products: 252 us -> none  [the longest x2 209 us: channel_block(): jnp.einsum('bse,ec->bsc', a_act, w_out, preferred_element_type=jnp.float32)]
    convert_element_type x7 -> x0, local copies, waits for them, and re-layouts: 245 us -> none  [the longest x2 91.7 us: local_layers(): t_cols = (t_sum + b_tok2[layer_idx][None, :, None]).astype(jnp.bfloat16)]
    all_to_all x1 -> x0, blocking collectives: 187 us -> none  [local_layers(): lax.all_to_all(u_norm, 'seq', split_axis=2, concat_axis=1, tiled=True)]
    reduce_scatter x0 -> x8, waiting for transfers between devices: none -> 175 us  [local_layers(): part = lax.psum_scatter(h, 'seq', scatter_dimension=1, tiled=True)]
    unnamed x43 -> x30, local copies, waits for them, and re-layouts: 155 us -> 12.7 us
    all_to_all x4 -> x0, local copies, waits for them, and re-layouts: 90.4 us -> none  [local_layers(): lax.all_to_all(u_norm, 'seq', split_axis=2, concat_axis=1, tiled=True)]
  transfers between devices with their start and end apart: 3 -> 16, of which waited for: 3 -> 8; matrix products, arithmetic and copies ran while one was open for 0% -> 2% of each run, Pallas kernels for 0% -> 45%
where the time goes in v1:
time: 584 us; the launch traced here: 582 us
  Pallas kernels  304 us (52%)
  waiting for transfers between devices  206 us (35%)
  local copies, waits for them, and re-layouts  36.2 us (6%)
  other arithmetic  20.5 us (4%)
  between operations  13.5 us (2%)
    pallas_call x8, Pallas kernels, rest(): pl.pallas_call(body, grid=(size,), out_shape=outs, in_specs=specs, out_sp...  268 us
    reduce_scatter x8, waiting for transfers between devices, local_layers(): part = lax.psum_scatter(h, 'seq', scatter_dimension=1, tiled=True)  175 us
    pallas_call x4, Pallas kernels, first(): pl.pallas_call(first_kernel, grid=(size,), out_shape=jax.ShapeDtypeStruct...  36 us
    all_gather x8, waiting for transfers between devices, local_layers(): gs.append(lax.all_gather(g, 'seq', axis=1, tiled=True))  26.6 us
    concatenate x1, other arithmetic, local_layers(): return jnp.concatenate(xs, 0)  14.1 us
    unnamed x30, local copies, waits for them, and re-layouts  12.7 us
    slice x1, local copies, waits for them, and re-layouts, local_layers(): xs = [x[c * size:(c + 1) * size] for c in range(CHUNKS)]  12.2 us
  transfers between devices with their start and end apart: 16, of which 8 were waited for; matrix products, arithmetic and copies ran while one was open for 2% of the time, Pallas kernels for 45%

profile of v1, /device:TPU:112, one launch (start us, length us, event | category | flops | bytes accessed | tf_op | source)
XLA Modules:
  0.0 581.8 jit_solution(18340815871422672582)
XLA Ops:
  6.6 0.7 slice_bitcast_fusion.4
  7.3 12.2 %fusion.64 = (bf16[8,512,512]{2,1,0:T(8,128)(2,1)}, bf16[8,512,512]{2,1,0:T(8,128)(2,1)}, bf16[8,512,512]{2,1,0:T(8,128)(2,1)}, bf16[8,512,512]{2,1,0:T(8,128)(2,1)}) fusion(bf16[32,512,512]{2,1,0:T(8,128)(2,1)} %param.10), kind=kLoop, calls=%fused_computation.88 | loop fusion | bytes 33554432 | tf_op jit(solution)/shard_map/slice | solution.py:120
  19.5 1.1 dynamic-slice_bitcast_fusion.1
  20.6 9.0 %shard_map.103 = f32[8,256,512]{2,1,0:T(8,128)} custom-call(bf16[8,512,512]{2,1,0:T(8,128)(2,1)} %get-tuple-element.22.x_ref, bf16[512,256]{1,0:T(8,128)(2,1)S(1)} %get-tuple-element.32.w1_ref, f32[4,512]{1,0:T(4,128)S(1)} %get-tuple-element.38.ln_ref), custom_call_target="tpu_custom_call" | custom-call | flops 1073741824 | bytes 8388608 | tf_op jit(solution)/shard_map/pallas_call | solution.py:86
  29.6 0.1 reduce-scatter.13.cloned.1.call-update
  29.6 0.1 reduce-scatter.17.cloned.1.call-start
  29.7 9.0 %shard_map.106 = f32[8,256,512]{2,1,0:T(8,128)} custom-call(bf16[8,512,512]{2,1,0:T(8,128)(2,1)} %get-tuple-element.24.x_ref, bf16[512,256]{1,0:T(8,128)(2,1)S(1)} %get-tuple-element.32.w1_ref, f32[4,512]{1,0:T(4,128)S(1)} %get-tuple-element.38.ln_ref), custom_call_target="tpu_custom_call" | custom-call | flops 1073741824 | bytes 8388608 | tf_op jit(solution)/shard_map/pallas_call | solution.py:86
  38.7 0.1 reduce-scatter.21.cloned.1.call-start
  38.8 9.0 %shard_map.109 = f32[8,256,512]{2,1,0:T(8,128)} custom-call(bf16[8,512,512]{2,1,0:T(8,128)(2,1)} %get-tuple-element.23.x_ref, bf16[512,256]{1,0:T(8,128)(2,1)S(1)} %get-tuple-element.32.w1_ref, f32[4,512]{1,0:T(4,128)S(1)} %get-tuple-element.38.ln_ref), custom_call_target="tpu_custom_call" | custom-call | flops 1073741824 | bytes 8388608 | tf_op jit(solution)/shard_map/pallas_call | solution.py:86
  47.9 0.1 reduce-scatter.9.cloned.1.call-start
  48.0 9.0 %shard_map.100 = f32[8,256,512]{2,1,0:T(8,128)} custom-call(bf16[8,512,512]{2,1,0:T(8,128)(2,1)} %get-tuple-element.21.x_ref, bf16[512,256]{1,0:T(8,128)(2,1)S(1)} %get-tuple-element.32.w1_ref, f32[4,512]{1,0:T(4,128)S(1)} %get-tuple-element.38.ln_ref), custom_call_target="tpu_custom_call" | custom-call | flops 1073741824 | bytes 8388608 | tf_op jit(solution)/shard_map/pallas_call | solution.py:86
  57.0 0.1 all-gather.17.cloned.1.call-start
  57.1 0.1 constant_dynamic-slice_fusion
  57.2 9.4 %reduce-scatter.13.cloned.1.call-done = f32[8,32,512]{2,1,0:T(8,128)} async-done(((f32[8,256,512]{2,1,0:T(8,128)}), f32[8,32,512]{2,1,0:T(8,128)}) %reduce-scatter.13.cloned.1.call-update) | async-done | bytes 524304 | tf_op jit(solution)/shard_map/reduce_scatter | solution.py:125
  66.6 35.1 %reduce-scatter.17.cloned.1.call-done = f32[8,32,512]{2,1,0:T(8,128)} async-done(((f32[8,256,512]{2,1,0:T(8,128)}), f32[8,32,512]{2,1,0:T(8,128)}) %reduce-scatter.17.cloned.1.call-update) | async-done | bytes 524304 | tf_op jit(solution)/shard_map/reduce_scatter | solution.py:125
  101.7 35.0 %reduce-scatter.21.cloned.1.call-done = f32[8,32,512]{2,1,0:T(8,128)} async-done(((f32[8,256,512]{2,1,0:T(8,128)}), f32[8,32,512]{2,1,0:T(8,128)}) %reduce-scatter.21.cloned.1.call-update) | async-done | bytes 524304 | tf_op jit(solution)/shard_map/reduce_scatter | solution.py:125
  136.8 34.9 %reduce-scatter.9.cloned.1.call-done = f32[8,32,512]{2,1,0:T(8,128)} async-done(((f32[8,256,512]{2,1,0:T(8,128)}), f32[8,32,512]{2,1,0:T(8,128)}) %reduce-scatter.9.cloned.1.call-update) | async-done | bytes 524304 | tf_op jit(solution)/shard_map/reduce_scatter | solution.py:125
  171.7 3.2 fusion.7
  174.9 0.1 all-gather.13.cloned.1.call-start
  175.0 0.6 all-gather.13.cloned.1.call-update
  175.5 0.1 all-gather.9.cloned.1.call-start
  175.6 0.7 all-gather.9.cloned.1.call-update
  176.3 0.1 all-gather.21.cloned.1.call-start
  176.4 0.7 all-gather.21.cloned.1.call-update
  177.2 0.1 reduce-scatter.19.cloned.1.call-start
  177.2 0.8 dynamic-slice_bitcast_fusion.4
  178.1 0.1 copy.11.b2_ref
  178.2 1.1 dynamic-slice_bitcast_fusion
  179.4 4.6 slice_bitcast_fusion
  184.0 2.5 slice_bitcast_fusion.1
  186.5 8.4 %all-gather.17.cloned.1.call-done.g_ref = bf16[8,256,512]{2,1,0:T(8,128)(2,1)} async-done(((bf16[8,32,512]{2,1,0:T(8,128)(2,1)}), bf16[8,256,512]{2,1,0:T(8,128)(2,1)}) %all-gather.17.cloned.1.call-update) | async-done | bytes 2097168 | tf_op jit(solution)/shard_map/all_gather | solution.py:127
  194.9 1.6 copy-done.5
  196.5 35.8 %shard_map.107 = (bf16[8,512,512]{2,1,0:T(8,128)(2,1)}, f32[8,256,512]{2,1,0:T(8,128)}) custom-call(bf16[8,512,512]{2,1,0:T(8,128)(2,1)} %get-tuple-element.24.x_ref, bf16[8,256,512]{2,1,0:T(8,128)(2,1)S(1)} %copy-done.5, bf16[256,512]{1,0:T(8,128)(2,1)S(1)} %get-tuple-element.30.w2_ref, f32[512,1]{1,0:T(8,128)S(1)} %copy.11.b2_ref, ...), custom_call_target="tpu_custom_call" | custom-call | flops 17179869184 | bytes 8388608 | tf_op jit(solution)/shard_map/pallas_call | solution.py:109
  232.3 0.2 reduce-scatter.15.cloned.1.call-start
  232.6 1.6 copy-done.4
  234.2 35.8 %shard_map.104 = (bf16[8,512,512]{2,1,0:T(8,128)(2,1)}, f32[8,256,512]{2,1,0:T(8,128)}) custom-call(bf16[8,512,512]{2,1,0:T(8,128)(2,1)} %get-tuple-element.22.x_ref, bf16[8,256,512]{2,1,0:T(8,128)(2,1)S(1)} %copy-done.4, bf16[256,512]{1,0:T(8,128)(2,1)S(1)} %get-tuple-element.30.w2_ref, f32[512,1]{1,0:T(8,128)S(1)} %copy.11.b2_ref, ...), custom_call_target="tpu_custom_call" | custom-call | flops 17179869184 | bytes 8388608 | tf_op jit(solution)/shard_map/pallas_call | solution.py:109
  270.1 0.1 reduce-scatter.11.cloned.1.call-start
  270.2 1.6 copy-done.3
  271.8 35.8 %shard_map.101 = (bf16[8,512,512]{2,1,0:T(8,128)(2,1)}, f32[8,256,512]{2,1,0:T(8,128)}) custom-call(bf16[8,512,512]{2,1,0:T(8,128)(2,1)} %get-tuple-element.21.x_ref, bf16[8,256,512]{2,1,0:T(8,128)(2,1)S(1)} %copy-done.3, bf16[256,512]{1,0:T(8,128)(2,1)S(1)} %get-tuple-element.30.w2_ref, f32[512,1]{1,0:T(8,128)S(1)} %copy.11.b2_ref, ...), custom_call_target="tpu_custom_call" | custom-call | flops 17179869184 | bytes 8388608 | tf_op jit(solution)/shard_map/pallas_call | solution.py:109
  307.7 0.1 reduce-scatter.23.cloned.1.call-start
  307.8 1.6 copy-done.2
  309.4 35.8 %shard_map.110 = (bf16[8,512,512]{2,1,0:T(8,128)(2,1)}, f32[8,256,512]{2,1,0:T(8,128)}) custom-call(bf16[8,512,512]{2,1,0:T(8,128)(2,1)} %get-tuple-element.23.x_ref, bf16[8,256,512]{2,1,0:T(8,128)(2,1)S(1)} %copy-done.2, bf16[256,512]{1,0:T(8,128)(2,1)S(1)} %get-tuple-element.30.w2_ref, f32[512,1]{1,0:T(8,128)S(1)} %copy.11.b2_ref, ...), custom_call_target="tpu_custom_call" | custom-call | flops 17179869184 | bytes 8388608 | tf_op jit(solution)/shard_map/pallas_call | solution.py:109
  345.2 0.1 all-gather.11.cloned.1.call-start
  345.3 25.9 %reduce-scatter.11.cloned.1.call-done = f32[8,32,512]{2,1,0:T(8,128)} async-done(((f32[8,256,512]{2,1,0:T(8,128)}), f32[8,32,512]{2,1,0:T(8,128)}) %reduce-scatter.11.cloned.1.call-update) | async-done | bytes 524304 | tf_op jit(solution)/shard_map/reduce_scatter | solution.py:125
  371.3 34.9 %reduce-scatter.23.cloned.1.call-done = f32[8,32,512]{2,1,0:T(8,128)} async-done(((f32[8,256,512]{2,1,0:T(8,128)}), f32[8,32,512]{2,1,0:T(8,128)}) %reduce-scatter.23.cloned.1.call-update) | async-done | bytes 524304 | tf_op jit(solution)/shard_map/reduce_scatter | solution.py:125
  406.1 3.2 fusion.15
  409.3 0.1 all-gather.11.cloned.1.call-update
  409.4 0.1 all-gather.15.cloned.1.call-start
  409.5 0.6 all-gather.15.cloned.1.call-update
  410.0 0.1 all-gather.19.cloned.1.call-start
  410.1 0.6 all-gather.19.cloned.1.call-update
  410.7 0.3 all-gather.23.cloned.1.call-start
  411.0 0.1 copy.12.b2_ref
  411.1 0.2 all-gather.23.cloned.1.call-update
  411.3 18.2 %all-gather.11.cloned.1.call-done.g_ref = bf16[8,256,512]{2,1,0:T(8,128)(2,1)} async-done(((bf16[8,32,512]{2,1,0:T(8,128)(2,1)}), bf16[8,256,512]{2,1,0:T(8,128)(2,1)}) %all-gather.11.cloned.1.call-update) | async-done | bytes 2097168 | tf_op jit(solution)/shard_map/all_gather | solution.py:127
  429.5 1.6 copy-done.6
  431.1 31.3 %shard_map.102 = bf16[8,512,512]{2,1,0:T(8,128)(2,1)} custom-call(bf16[8,512,512]{2,1,0:T(8,128)(2,1)} %get-tuple-element.13.x_ref, bf16[8,256,512]{2,1,0:T(8,128)(2,1)S(1)} %copy-done.6, bf16[256,512]{1,0:T(8,128)(2,1)S(1)} %get-tuple-element.29.w2_ref, f32[512,1]{1,0:T(8,128)S(1)} %copy.12.b2_ref, bf16[512,2048]{1,0:T(8,128)(2,1)} %get-tuple-element.27.wc1_ref, ...), custom_call_target="tpu_custom_call" | custom-call | flops 17179869184 | bytes 8388608 | tf_op jit(solution)/shard_map/pallas_call | solution.py:109
  462.3 1.6 copy-done.7
  463.9 31.2 %shard_map.105 = bf16[8,512,512]{2,1,0:T(8,128)(2,1)} custom-call(bf16[8,512,512]{2,1,0:T(8,128)(2,1)} %get-tuple-element.15.x_ref, bf16[8,256,512]{2,1,0:T(8,128)(2,1)S(1)} %copy-done.7, bf16[256,512]{1,0:T(8,128)(2,1)S(1)} %get-tuple-element.29.w2_ref, f32[512,1]{1,0:T(8,128)S(1)} %copy.12.b2_ref, bf16[512,2048]{1,0:T(8,128)(2,1)} %get-tuple-element.27.wc1_ref, ...), custom_call_target="tpu_custom_call" | custom-call | flops 17179869184 | bytes 8388608 | tf_op jit(solution)/shard_map/pallas_call | solution.py:109
  495.2 1.6 copy-done.9
  496.8 31.3 %shard_map.108 = bf16[8,512,512]{2,1,0:T(8,128)(2,1)} custom-call(bf16[8,512,512]{2,1,0:T(8,128)(2,1)} %get-tuple-element.17.x_ref, bf16[8,256,512]{2,1,0:T(8,128)(2,1)S(1)} %copy-done.9, bf16[256,512]{1,0:T(8,128)(2,1)S(1)} %get-tuple-element.29.w2_ref, f32[512,1]{1,0:T(8,128)S(1)} %copy.12.b2_ref, bf16[512,2048]{1,0:T(8,128)(2,1)} %get-tuple-element.27.wc1_ref, ...), custom_call_target="tpu_custom_call" | custom-call | flops 17179869184 | bytes 8388608 | tf_op jit(solution)/shard_map/pallas_call | solution.py:109
  528.0 1.6 copy-done.8
  529.6 31.4 %shard_map.111 = bf16[8,512,512]{2,1,0:T(8,128)(2,1)} custom-call(bf16[8,512,512]{2,1,0:T(8,128)(2,1)} %get-tuple-element.19.x_ref, bf16[8,256,512]{2,1,0:T(8,128)(2,1)S(1)} %copy-done.8, bf16[256,512]{1,0:T(8,128)(2,1)S(1)} %get-tuple-element.29.w2_ref, f32[512,1]{1,0:T(8,128)S(1)} %copy.12.b2_ref, bf16[512,2048]{1,0:T(8,128)(2,1)} %get-tuple-element.27.wc1_ref, ...), custom_call_target="tpu_custom_call" | custom-call | flops 17179869184 | bytes 8388608 | tf_op jit(solution)/shard_map/pallas_call | solution.py:109
  561.1 14.1 %pad_maximum_fusion = bf16[32,512,512]{2,1,0:T(8,128)(2,1)} fusion(bf16[8,512,512]{2,1,0:T(8,128)(2,1)} %shard_map.111, bf16[8,512,512]{2,1,0:T(8,128)(2,1)} %shard_map.108, bf16[8,512,512]{2,1,0:T(8,128)(2,1)S(1)} %copy-done.12, bf16[8,512,512]{2,1,0:T(8,128)(2,1)S(1)} %copy-done.11), kind=kLoop, calls=%fused_computation | loop fusion | flops 25165824 | bytes 33554432 | tf_op jit(solution)/shard_map/concatenate | solution.py:131
  (42 shorter events, 0.6 us)
Async XLA Ops:
  6.5 50.6 %copy-start = (f32[2,256]{1,0:T(2,128)S(1)}, f32[2,256]{1,0:T(2,128)}, u32[]{:S(2)}) copy-start(f32[2,256]{1,0:T(2,128)} %param.12) | copy-start | bytes 6148
  6.6 60.0 %reduce-scatter.13.cloned.1.call-start = ((), (), s32[]{:S(2)}) async-start(), calls=%async_computation.12 | async-start | bytes 4718592 | tf_op jit(solution)/shard_map/reduce_scatter | solution.py:125
  29.6 72.1 %reduce-scatter.17.cloned.1.call-start = ((), (), s32[]{:S(2)}) async-start(), calls=%async_computation.16 | async-start | bytes 4718592 | tf_op jit(solution)/shard_map/reduce_scatter | solution.py:125
  38.7 98.0 %reduce-scatter.21.cloned.1.call-start = ((), (), s32[]{:S(2)}) async-start(), calls=%async_computation.20 | async-start | bytes 4718592 | tf_op jit(solution)/shard_map/reduce_scatter | solution.py:125
  47.9 123.8 %reduce-scatter.9.cloned.1.call-start = ((), (), s32[]{:S(2)}) async-start(), calls=%async_computation.8 | async-start | bytes 4718592 | tf_op jit(solution)/shard_map/reduce_scatter | solution.py:125
  57.0 122.3 %copy-start.14 = (f32[2,512]{1,0:T(2,128)S(1)}, f32[2,512]{1,0:T(2,128)}, u32[]{:S(2)}) copy-start(f32[2,512]{1,0:T(2,128)} %param.18) | copy-start | bytes 12292
  57.0 122.4 %copy-start.13 = (f32[2,2048]{1,0:T(2,128)S(1)}, f32[2,2048]{1,0:T(2,128)}, u32[]{:S(2)}) copy-start(f32[2,2048]{1,0:T(2,128)} %param.16) | copy-start | bytes 49156
  57.0 137.9 %all-gather.17.cloned.1.call-start = ((), (), s32[]{:S(2)}) async-start(), calls=%async_computation.17 | async-start | bytes 2359296 | tf_op jit(solution)/shard_map/all_gather | solution.py:127
  174.9 57.7 %all-gather.13.cloned.1.call-start = ((), (), s32[]{:S(2)}) async-start(), calls=%async_computation.13 | async-start | bytes 2359296 | tf_op jit(solution)/shard_map/all_gather | solution.py:127
  175.5 94.7 %all-gather.9.cloned.1.call-start = ((), (), s32[]{:S(2)}) async-start(), calls=%async_computation.9 | async-start | bytes 2359296 | tf_op jit(solution)/shard_map/all_gather | solution.py:127
  176.3 131.4 %all-gather.21.cloned.1.call-start = ((), (), s32[]{:S(2)}) async-start(), calls=%async_computation.21 | async-start | bytes 2359296 | tf_op jit(solution)/shard_map/all_gather | solution.py:127
  177.2 168.1 %reduce-scatter.19.cloned.1.call-start = ((), (), s32[]{:S(2)}) async-start(), calls=%async_computation.18 | async-start | bytes 4718592 | tf_op jit(solution)/shard_map/reduce_scatter | solution.py:125
  179.4 4.6 copy-start.10
  194.9 1.6 copy-start.5
  232.3 113.0 %reduce-scatter.15.cloned.1.call-start = ((), (), s32[]{:S(2)}) async-start(), calls=%async_computation.14 | async-start | bytes 4718592 | tf_op jit(solution)/shard_map/reduce_scatter | solution.py:125
  232.6 1.6 copy-start.4
  270.1 101.2 %reduce-scatter.11.cloned.1.call-start = ((), (), s32[]{:S(2)}) async-start(), calls=%async_computation.10 | async-start | bytes 4718592 | tf_op jit(solution)/shard_map/reduce_scatter | solution.py:125
  270.2 1.6 copy-start.3
  307.7 98.4 %reduce-scatter.23.cloned.1.call-start = ((), (), s32[]{:S(2)}) async-start(), calls=%async_computation.22 | async-start | bytes 4718592 | tf_op jit(solution)/shard_map/reduce_scatter | solution.py:125
  307.8 1.6 copy-start.2
  345.2 84.3 %all-gather.11.cloned.1.call-start = ((), (), s32[]{:S(2)}) async-start(), calls=%async_computation.11 | async-start | bytes 2359296 | tf_op jit(solution)/shard_map/all_gather | solution.py:127
  409.4 52.9 %all-gather.15.cloned.1.call-start = ((), (), s32[]{:S(2)}) async-start(), calls=%async_computation.15 | async-start | bytes 2359296 | tf_op jit(solution)/shard_map/all_gather | solution.py:127
  410.0 85.1 %all-gather.19.cloned.1.call-start = ((), (), s32[]{:S(2)}) async-start(), calls=%async_computation.19 | async-start | bytes 2359296 | tf_op jit(solution)/shard_map/all_gather | solution.py:127
  410.7 117.4 %all-gather.23.cloned.1.call-start = ((), (), s32[]{:S(2)}) async-start(), calls=%async_computation.23 | async-start | bytes 2359296 | tf_op jit(solution)/shard_map/all_gather | solution.py:127
  429.5 1.6 copy-start.6
  462.3 1.6 copy-start.7
  495.2 1.6 copy-start.9
  528.0 1.6 copy-start.8
  529.6 31.5 %copy-start.11 = (bf16[8,512,512]{2,1,0:T(8,128)(2,1)S(1)}, bf16[8,512,512]{2,1,0:T(8,128)(2,1)}, u32[]{:S(2)}) copy-start(bf16[8,512,512]{2,1,0:T(8,128)(2,1)} %shard_map.102) | copy-start | bytes 12582916
  529.6 31.5 %copy-start.12 = (bf16[8,512,512]{2,1,0:T(8,128)(2,1)S(1)}, bf16[8,512,512]{2,1,0:T(8,128)(2,1)}, u32[]{:S(2)}) copy-start(bf16[8,512,512]{2,1,0:T(8,128)(2,1)} %shard_map.105) | copy-start | bytes 12582916
  561.1 14.1 %copy-start.1 = (f32[2,256]{1,0:T(2,128)S(1)}, f32[2,256]{1,0:T(2,128)}, u32[]{:S(2)}) copy-start(f32[2,256]{1,0:T(2,128)} %param.12) | copy-start | bytes 6148
Sparse Core Ops, SparseCore 0:
  29.8 36.7 reduce-scatter.12
  68.9 32.7 reduce-scatter.16
  104.0 32.6 reduce-scatter.20
  138.9 32.7 reduce-scatter.8
  175.0 19.8 all-gather.16
  196.3 21.5 all-gather.12
  219.5 21.5 all-gather.8
  242.7 21.5 all-gather.20
  266.6 34.4 reduce-scatter.18
  303.3 32.7 reduce-scatter.14
  338.5 32.7 reduce-scatter.10
  373.4 32.6 reduce-scatter.22
  409.5 19.9 all-gather.10
  430.9 21.5 all-gather.14
  453.9 21.5 all-gather.18
  477.0 21.5 all-gather.22

commit v2 on v0

v2 whole, which is shorter than its diff:
```python
import functools

import jax
import jax.numpy as jnp
from jax import lax
from jax.experimental import pallas as pl
from jax.experimental.pallas import tpu as pltpu
from jax.sharding import PartitionSpec as P

F32 = jnp.float32
BF16 = jnp.bfloat16
MESH = pl.DeviceIdType.MESH
LN_EPS = 1e-6
GELU_A = 0.7978845608028654
GELU_B = GELU_A * 0.044715

GROUP = 2
SLOTS = 10
HELD = 4
LAG = 12
WIDTH = 256
STRIP = 32

P1, M1L, M1R, M2L, M2R, GL, GR, GP, FL, FR, PA, PB, PC = range(13)
KINDS = 13


def dot(a, b):
    return jnp.dot(a, b, preferred_element_type=F32)


def gelu(h):
    return 0.5 * h * (1.0 + jnp.tanh(h * (GELU_A + GELU_B * (h * h))))


def gelu_of_half(h):
    return h + h * jnp.tanh(h * (2.0 * GELU_A + (8.0 * GELU_B) * (h * h)))


def norm(rows, scale, offset):
    rows = rows.astype(F32)
    mean = jnp.mean(rows, axis=-1, keepdims=True)
    centered = rows - mean
    var = jnp.mean(centered * centered, axis=-1, keepdims=True)
    return (centered * lax.rsqrt(var + LN_EPS) * scale + offset).astype(BF16)


def kernel(chips, x_hbm, w1, w2, b1, b2, wc1_hbm, bc1, wc2_hbm, bc2, ln, z_hbm,
           xb, wc1, wc2, act, v0, v1, tb, ub, hpart, pbuf, cbuf, m1, m2, gall,
           xsem, wsem, zsem, ssem, rsem):
    batch, rows, chans = x_hbm.shape
    layers = w1.shape[0]
    wide = wc1.shape[2]
    groups = batch // GROUP
    items = layers * groups
    own = gall.shape[3]
    half = own // 2

    me = lax.axis_index("seq")
    chip, core = lax.div(me, 2), lax.rem(me, 2)
    right = lax.rem(chip + 1, chips)
    left = lax.rem(chip + chips - 1, chips)
    far = lax.rem(chip + 2, chips)
    dev_right, dev_left, dev_pair = 2 * right + core, 2 * left + core, 2 * chip + (1 - core)
    mine = core * chips
    other = (1 - core) * chips

    barrier = pltpu.get_barrier_semaphore()
    for dev in (dev_left, dev_right, dev_pair):
        pl.semaphore_signal(barrier, inc=1, device_id={"seq": dev}, device_id_type=MESH)
    pl.semaphore_wait(barrier, 3)

    def load_x(g):
        at = pl.ds(g * GROUP, GROUP)
        return pltpu.make_async_copy(x_hbm.at[at], xb.at[at], xsem.at[g])

    def store_z(g):
        at = pl.ds(g * GROUP, GROUP)
        return pltpu.make_async_copy(xb.at[at], z_hbm.at[at], zsem.at[g])

    def weight_copies():
        return (pltpu.make_async_copy(wc1_hbm, wc1, wsem.at[0]), pltpu.make_async_copy(wc2_hbm, wc2, wsem.at[1]))

    for g in range(groups):
        load_x(g).start()
    for c in weight_copies():
        c.start()

    def remote(kind, slot, dev, src, dst):
        return pltpu.make_async_remote_copy(
            src_ref=src, dst_ref=dst, send_sem=ssem.at[kind, slot], recv_sem=rsem.at[kind, slot],
            device_id={"seq": dev}, device_id_type=MESH)

    def stage(s, lag, fn):
        i = s - lag

        @pl.when((i >= 0) & (i < items))
        def _():
            fn(i, lax.rem(i, SLOTS))

    def wait(kind, slot, dev, region):
        c = remote(kind, slot, dev, region, region)
        c.wait_recv()
        c.wait_send()

    def exchange(s):
        def send_pair(i, sl):
            remote(P1, sl, dev_pair, hpart.at[lax.rem(i, HELD), :, 1 - core], pbuf.at[sl]).start()

        def chip_sum(i, sl):
            wait(P1, sl, dev_pair, pbuf.at[sl])
            for g in range(GROUP):
                cbuf[sl, g] = hpart[lax.rem(i, HELD), g, core] + pbuf[sl, g]
            remote(M1L, sl, dev_right, cbuf.at[sl, :, far, pl.ds(0, half)], m1.at[sl, 0]).start()
            remote(M1R, sl, dev_left, cbuf.at[sl, :, far, pl.ds(half, half)], m1.at[sl, 1]).start()

        def pass_sums(i, sl):
            wait(M1L, sl, dev_right, m1.at[sl, 0])
            wait(M1R, sl, dev_left, m1.at[sl, 1])
            for g in range(GROUP):
                cbuf[sl, g, right, 0:half] = cbuf[sl, g, right, 0:half] + m1[sl, 0, g]
                cbuf[sl, g, left, half:own] = cbuf[sl, g, left, half:own] + m1[sl, 1, g]
            remote(M2L, sl, dev_right, cbuf.at[sl, :, right], m2.at[sl, 0]).start()
            remote(M2R, sl, dev_left, cbuf.at[sl, :, left], m2.at[sl, 1]).start()

        def finish_sums(i, sl):
            wait(M2L, sl, dev_right, m2.at[sl, 0])
            wait(M2R, sl, dev_left, m2.at[sl, 1])
            bias = b1[lax.div(i, groups)]
            for g in range(GROUP):
                h = (cbuf[sl, g, chip] + m2[sl, 0, g]) + m2[sl, 1, g] + bias
                gall[sl, g, mine + chip] = gelu(h).astype(BF16)
            block = gall.at[sl, :, mine + chip]
            remote(GL, sl, dev_right, block, block).start()
            remote(GR, sl, dev_left, block, block).start()
            remote(GP, sl, dev_pair, block, block).start()

        def forward(i, sl):
            from_left, from_right = gall.at[sl, :, mine + left], gall.at[sl, :, mine + right]
            wait(GL, sl, dev_right, from_left)
            wait(GR, sl, dev_left, from_right)
            wait(GP, sl, dev_pair, gall.at[sl, :, other + chip])
            a = gall.at[sl, :, mine + left, pl.ds(0, half)]
            b = gall.at[sl, :, mine + right, pl.ds(half, half)]
            remote(FL, sl, dev_right, a, a).start()
            remote(FR, sl, dev_left, b, b).start()
            remote(PA, sl, dev_pair, from_left, from_left).start()
            remote(PB, sl, dev_pair, from_right, from_right).start()

        def forward_far(i, sl):
            wait(FL, sl, dev_right, gall.at[sl, :, mine + far, pl.ds(0, half)])
            wait(FR, sl, dev_left, gall.at[sl, :, mine + far, pl.ds(half, half)])
            wait(PA, sl, dev_pair, gall.at[sl, :, other + left])
            wait(PB, sl, dev_pair, gall.at[sl, :, other + right])
            block = gall.at[sl, :, mine + far]
            remote(PC, sl, dev_pair, block, block).start()

        def complete(i, sl):
            wait(PC, sl, dev_pair, gall.at[sl, :, other + far])

        stage(s, 1, send_pair)
        stage(s, 2, chip_sum)
        stage(s, 4, pass_sums)
        stage(s, 6, finish_sums)
        stage(s, 8, forward)
        stage(s, 10, forward_far)
        stage(s, 11, complete)

    def unit(s, j, do_a, do_b, do_c, do_h):
        v_cur, v_next = (v0, v1) if j % 2 == 0 else (v1, v0)
        qa = (s - LAG) * GROUP + j
        qb, qc = qa - 1, qa + 1
        if do_a:
            la = lax.div(qa, batch)
        if do_b:
            lb = lax.div(jnp.maximum(qb, 0), batch)
            ib = jnp.where(qb < 0, batch, lax.rem(jnp.maximum(qb, 0), batch))
        if do_c:
            lc = jnp.minimum(lax.div(qc, batch), layers - 1)
            ic = jnp.where(qc >= items * GROUP, batch, lax.rem(qc, batch))
            gc = gall[lax.rem(lax.div(qc, GROUP), SLOTS), lax.rem(qc, GROUP)].reshape(2 * chips * own, chans)
            tb[...] = (dot(w2[lc], gc) + b2[lc]).astype(BF16)
        if do_h:
            lh = lax.div(s, groups)
            ih = lax.rem(s, groups) * GROUP + j
        blocks = wide // WIDTH
        share = rows // blocks
        acc = None
        for k in range(blocks):
            cols = slice(k * WIDTH, (k + 1) * WIDTH)
            if do_b:
                part = dot(act[:, cols], wc2[lb, cols, :])
                acc = part if acc is None else acc + part
            if do_a:
                act[:, cols] = gelu_of_half(dot(v_cur[...], wc1[la, :, cols]) + bc1[la, :, cols]).astype(BF16)
            for r in range(k * share, (k + 1) * share, STRIP):
                strip = slice(r, r + STRIP)
                if do_c:
                    x1 = xb[ic, strip] + tb[strip]
                if do_h:
                    xh = xb[ih, strip]
                if do_c:
                    xb[ic, strip] = x1
                    v_next[strip] = norm(x1, ln[lc, 2:3], ln[lc, 3:4])
                if do_h:
                    ub[strip] = norm(xh, ln[lh, 0:1], ln[lh, 1:2])
        if do_b:
            xb[ib] = (xb[ib].astype(F32) + (acc + bc2[lb])).astype(BF16)
        if do_h:
            hpart[lax.rem(s, HELD), j] = dot(w1[lh], ub[...]).reshape(2, chips, own, chans)

    def finished(s):
        i = s - LAG - 1 - (layers - 1) * groups

        @pl.when((i >= 0) & (i < groups))
        def _():
            store_z(i).start()

    def units(s, *parts):
        for j in range(GROUP):
            unit(s, j, *parts)
            if j == 0 and parts[1]:
                finished(s)

    def step(s, carry):
        exchange(s)

        @pl.when(s < groups)
        def _():
            load_x(s).wait()

        @pl.when(s == LAG // 2)
        def _():
            for c in weight_copies():
                c.wait()

            def scale(r, carry):
                at = pl.ds(pl.multiple_of(r * 64, 64), 64)
                for l in range(layers):
                    wc1[l, at] = wc1[l, at] * jnp.asarray(0.5, BF16)
                return carry

            lax.fori_loop(0, chans // 64, scale, 0)

        @pl.when(s < LAG)
        def _():
            units(s, False, False, False, True)

        @pl.when(s == LAG - 1)
        def _():
            unit(s, GROUP - 1, False, False, True, False)

        @pl.when((s >= LAG) & (s < items))
        def _():
            units(s, True, True, True, True)

        @pl.when((s >= items) & (s < items + LAG))
        def _():
            units(s, True, True, True, False)

        @pl.when(s == items + LAG)
        def _():
            unit(s, 0, False, True, False, False)
            finished(s)

        return carry

    lax.fori_loop(0, items + LAG + 1, step, 0)

    def drain(g, carry):
        store_z(g).wait()
        return carry

    lax.fori_loop(0, groups, drain, 0)


def solution(mesh):
    size = mesh.shape["seq"]
    chips = size // 2

    def local_layers(x, w_tok1, b_tok1, w_tok2, b_tok2, w_ch1, b_ch1, w_ch2, b_ch2, ln_params):
        layers = w_tok1.shape[0]
        batch, rows, chans = x.shape
        hid, wide = w_tok1.shape[2], w_ch1.shape[2]
        own = hid // size
        groups = batch // GROUP
        me = lax.axis_index("seq")
        w1 = lax.dynamic_slice_in_dim(w_tok1, me * rows, rows, 1).transpose(0, 2, 1)
        w2 = lax.dynamic_slice_in_dim(w_tok2, me * rows, rows, 2).transpose(0, 2, 1)
        b2 = lax.dynamic_slice_in_dim(b_tok2, me * rows, rows, 1)[:, :, None]
        first = ((me % 2) * chips + me // 2) * own
        b1 = lax.dynamic_slice_in_dim(b_tok1, first, own, 1)[:, :, None]
        vmem = pl.BlockSpec(memory_space=pltpu.VMEM)
        hbm = pl.BlockSpec(memory_space=pl.ANY)
        tile = pltpu.VMEM((rows, chans), BF16)
        return pl.pallas_call(
            functools.partial(kernel, chips),
            out_shape=jax.ShapeDtypeStruct(x.shape, BF16),
            in_specs=[hbm, vmem, vmem, vmem, vmem, hbm, vmem, hbm, vmem, vmem],
            out_specs=hbm,
            scratch_shapes=[
                pltpu.VMEM((batch + 1, rows, chans), BF16),
                pltpu.VMEM(w_ch1.shape, BF16),
                pltpu.VMEM(w_ch2.shape, BF16),
                pltpu.VMEM((rows, wide), BF16),
                tile, tile, tile, tile,
                pltpu.VMEM((HELD, GROUP, 2, chips, own, chans), F32),
                pltpu.VMEM((SLOTS, GROUP, chips, own, chans), F32),
                pltpu.VMEM((SLOTS, GROUP, chips, own, chans), F32),
                pltpu.VMEM((SLOTS, 2, GROUP, own // 2, chans), F32),
                pltpu.VMEM((SLOTS, 2, GROUP, own, chans), F32),
                pltpu.VMEM((SLOTS, GROUP, 2 * chips, own, chans), BF16),
                pltpu.SemaphoreType.DMA((groups,)),
                pltpu.SemaphoreType.DMA((2,)),
                pltpu.SemaphoreType.DMA((groups,)),
                pltpu.SemaphoreType.DMA((KINDS, SLOTS)),
                pltpu.SemaphoreType.DMA((KINDS, SLOTS)),
            ],
            compiler_params=pltpu.CompilerParams(
                collective_id=0, has_side_effects=True, vmem_limit_bytes=67043328),
        )(x, w1, w2, b1, b2, w_ch1, 0.5 * b_ch1[:, None], w_ch2, b_ch2[:, None], ln_params)

    act = P("data", "seq", None)
    rep = P()
    return jax.shard_map(local_layers, mesh=mesh, in_specs=(act,) + (rep,) * 9, out_specs=act, check_vma=False)
```

time: 1600 us -> 279 us (0.17); the launches traced: 1580 us -> 278 us
  waiting for transfers between devices: 547 us -> 0 us
  local copies, waits for them, and re-layouts: 497 us -> 23 us
  Pallas kernels: 0 us -> 255 us
  matrix products: 252 us -> 0 us
  blocking collectives: 187 us -> 0 us
  other arithmetic: 80.1 us -> 0.72 us
  starting transfers between devices: 18.2 us -> 0 us
    all_to_all x3 -> x0, waiting for transfers between devices: 547 us -> none  [the longest x2 364 us: local_layers(): lax.all_to_all(t_cols, 'seq', split_axis=1, concat_axis=2, tiled=True)]
    pallas_call x0 -> x1, Pallas kernels: none -> 255 us  [local_layers(): pl.pallas_call(functools.partial(kernel, chips), out_shape=jax.ShapeDtype...]
    dot_general x6 -> x0, matrix products: 252 us -> none  [the longest x2 209 us: channel_block(): jnp.einsum('bse,ec->bsc', a_act, w_out, preferred_element_type=jnp.float32)]
    convert_element_type x7 -> x0, local copies, waits for them, and re-layouts: 245 us -> none  [the longest x2 91.7 us: local_layers(): t_cols = (t_sum + b_tok2[layer_idx][None, :, None]).astype(jnp.bfloat16)]
    all_to_all x1 -> x0, blocking collectives: 187 us -> none  [local_layers(): lax.all_to_all(u_norm, 'seq', split_axis=2, concat_axis=1, tiled=True)]
    unnamed x43 -> x3, local copies, waits for them, and re-layouts: 155 us -> 15.8 us
    all_to_all x4 -> x0, local copies, waits for them, and re-layouts: 90.4 us -> none  [local_layers(): lax.all_to_all(u_norm, 'seq', split_axis=2, concat_axis=1, tiled=True)]
    reduce_sum x7 -> x0, other arithmetic: 65 us -> none  [the longest x3 42.1 us: layer_norm(): row_mean = jnp.mean(row_vals, axis=-1, keepdims=True)]
  transfers between devices with their start and end apart: 3 -> 0, of which waited for: 3 -> 0; matrix products, arithmetic and copies ran while one was open for 0% -> 0% of each run, Pallas kernels for 0% -> 0%
where the time goes in v2:
time: 279 us; the launch traced here: 278 us
  Pallas kernels  255 us (91%)
  local copies, waits for them, and re-layouts  23 us (8%)
    pallas_call x1, Pallas kernels, local_layers(): pl.pallas_call(functools.partial(kernel, chips), out_shape=jax.ShapeDtype...  255 us
    unnamed x3, local copies, waits for them, and re-layouts  15.8 us

profile of v2, /device:TPU:112, one launch (start us, length us, event | category | flops | bytes accessed | tf_op | source)
XLA Modules:
  0.0 278.4 jit_solution(5115520031261543445)
XLA Ops:
  0.0 0.7 dynamic-slice_bitcast_fusion.1
  0.8 0.7 dynamic-slice_bitcast_fusion
  1.4 1.3 broadcast_in_dim.12.bc2
  2.7 0.7 broadcast_multiply_fusion
  3.4 0.6 mul.24.bc1
  4.1 0.7 copy.16.b1
  4.7 1.0 copy.17.b2
  5.8 1.1 constant_dynamic-slice_fusion.1
  6.9 1.0 copy.18
  7.9 1.1 constant_dynamic-slice_fusion
  8.9 1.0 copy.19
  9.9 254.6 %shard_map.100 = bf16[32,512,512]{2,1,0:T(8,128)(2,1)} custom-call(bf16[32,512,512]{2,1,0:T(8,128)(2,1)} %x_hbm.1, bf16[2,256,512]{2,1,0:T(8,128)(2,1)} %bitcast.6, bf16[2,512,256]{2,1,0:T(8,128)(2,1)} %bitcast.7, f32[2,32,1]{2,1,0:T(8,128)} %copy.16.b1, f32[2,512,1]{2,1,0:T(8,128)} %copy.17.b2, bf16[2,512,2048]{2,1,0:T(8,128)(2,1)} %wc1_hbm.1, ...), custom_call_target="tpu_custom_call" | custom-call | tf_op jit(solution)/shard_map/pallas_call | solution.py:296
  264.6 13.8 %copy.21 = bf16[32,512,512]{2,1,0:T(8,128)(2,1)} copy(bf16[32,512,512]{2,1,0:T(8,128)(2,1)} %shard_map.100) | data formatting | bytes 33554432

commit v3 on v2

v3 whole, which is shorter than its diff:
```python
import functools

import jax
import jax.numpy as jnp
from jax import lax
from jax.experimental import pallas as pl
from jax.experimental.pallas import tpu as pltpu
from jax.sharding import PartitionSpec as P

F32 = jnp.float32
BF16 = jnp.bfloat16
MESH = pl.DeviceIdType.MESH
LN_EPS = 1e-6
GELU_A = 0.7978845608028654
GELU_B = GELU_A * 0.044715

GROUP = 2
SLOTS = 9
HELD = 2
LAG = 15
WIDTH = 256
STRIP = 32

P1, M1L, M1R, M2L, M2R, GL, GR, GP, FL, FR, PX = range(11)
KINDS = 11
OWN, RIGHT, LEFT, FAR = range(4)
MINE, OTHER = range(2)
LEFT_OVER = 2


def dot(a, b):
    return jnp.dot(a, b, preferred_element_type=F32)


def gelu(h):
    return 0.5 * h * (1.0 + jnp.tanh(h * (GELU_A + GELU_B * (h * h))))


def gelu_of_half(h):
    return h + h * jnp.tanh(h * (2.0 * GELU_A + (8.0 * GELU_B) * (h * h)))


def norm(rows, scale, offset):
    rows = rows.astype(F32)
    mean = jnp.mean(rows, axis=-1, keepdims=True)
    centered = rows - mean
    var = jnp.mean(centered * centered, axis=-1, keepdims=True)
    return (centered * lax.rsqrt(var + LN_EPS) * scale + offset).astype(BF16)


def column(row, offset, count):
    shape = (count, row.shape[1])
    hit = lax.broadcasted_iota(jnp.int32, shape, 1) == lax.broadcasted_iota(jnp.int32, shape, 0) + offset
    return jnp.sum(jnp.where(hit, row, 0.0), axis=1, keepdims=True)


def kernel(chips, x_hbm, w1_hbm, b1_row, w2_hbm, b2_row, wc1_hbm, bc1, wc2_hbm, bc2, ln, z_hbm,
           xb, wc1, wc2, act, v0, v1, tb, ub, hpart, pbuf, cbuf, m1, m2, gall, w1_raw, w2_raw, w1, w2, b1, b2,
           xsem, wsem, zsem, ssem, rsem):
    batch, rows, chans = x_hbm.shape
    layers = w1.shape[0]
    wide = wc1.shape[2]
    groups = batch // GROUP
    items = layers * groups
    last = items - LEFT_OVER
    stop = last * GROUP + LAG
    own = gall.shape[4]
    half = own // 2

    me = lax.axis_index("seq")
    chip, core = lax.div(me, 2), lax.rem(me, 2)
    right = lax.rem(chip + 1, chips)
    left = lax.rem(chip + chips - 1, chips)
    far = lax.rem(chip + 2, chips)
    dev_right, dev_left, dev_pair = 2 * right + core, 2 * left + core, 2 * chip + (1 - core)
    order = [(c * chips + k) * own for c in (core, 1 - core) for k in (chip, right, left, far)]

    def load_x(g):
        at = pl.ds(g * GROUP, GROUP)
        return pltpu.make_async_copy(x_hbm.at[at], xb.at[at], xsem.at[g])

    def store_z(g):
        at = pl.ds(g * GROUP, GROUP)
        return pltpu.make_async_copy(xb.at[at], z_hbm.at[at], zsem.at[g])

    def weight_copies():
        return (pltpu.make_async_copy(wc1_hbm, wc1, wsem.at[0]), pltpu.make_async_copy(wc2_hbm, wc2, wsem.at[1]))

    mixing_rows = pl.ds(pl.multiple_of(me * rows, rows), rows)
    rest = pl.ds(1, layers - 1)
    mixing = (pltpu.make_async_copy(w1_hbm.at[0, mixing_rows], w1_raw.at[0], wsem.at[2]),
              pltpu.make_async_copy(w1_hbm.at[rest, mixing_rows], w1_raw.at[rest], wsem.at[3]),
              pltpu.make_async_copy(w2_hbm.at[:, :, mixing_rows], w2_raw, wsem.at[4]))

    barrier = pltpu.get_barrier_semaphore()
    for dev in (dev_left, dev_right, dev_pair):
        pl.semaphore_signal(barrier, inc=1, device_id={"seq": dev}, device_id_type=MESH)
    mixing[0].start()
    load_x(0).start()

    hid = 2 * chips * own

    def place_w1(l):
        ub[0:hid] = w1_raw[l].T
        for n, at in enumerate(order):
            w1[l, n * own:(n + 1) * own] = ub[pl.ds(pl.multiple_of(at, own), own)]

    def place_rest():
        for l in range(1, layers):
            place_w1(l)
        for l in range(layers):
            for n, at in enumerate(order):
                tb[n * own:(n + 1) * own] = w2_raw[l, pl.ds(pl.multiple_of(at, own), own)]
            w2[l] = tb[0:hid].T
            b1[l] = column(b1_row[l:l + 1], order[0], own)
            for r in range(0, rows, 128):
                at = pl.ds(pl.multiple_of(me * rows + r, 128), 128)
                b2[l, r:r + 128] = column(b2_row[l:l + 1, at], 0, 128)

    mixing[0].wait()
    place_w1(0)
    for g in range(1, groups):
        load_x(g).start()
    for c in mixing[1:] + weight_copies():
        c.start()
    pl.semaphore_wait(barrier, 3)

    def remote(kind, slot, dev, src, dst):
        return pltpu.make_async_remote_copy(
            src_ref=src, dst_ref=dst, send_sem=ssem.at[kind, slot], recv_sem=rsem.at[kind, slot],
            device_id={"seq": dev}, device_id_type=MESH)

    def stage(s, lag, fn):
        i = s - lag

        @pl.when((i >= 0) & (i < items))
        def _():
            fn(i, lax.rem(i, SLOTS))

    def wait(kind, slot, dev, region):
        c = remote(kind, slot, dev, region, region)
        c.wait_recv()
        c.wait_send()

    def exchange(s, point):
        def send_pair(i, sl):
            remote(P1, sl, dev_pair, hpart.at[lax.rem(i, HELD), :, OTHER], pbuf.at[sl]).start()

        def chip_sum(i, sl):
            wait(P1, sl, dev_pair, pbuf.at[sl])
            for g in range(GROUP):
                cbuf[sl, g] = hpart[lax.rem(i, HELD), g, MINE] + pbuf[sl, g]
            remote(M1L, sl, dev_right, cbuf.at[sl, :, FAR, pl.ds(0, half)], m1.at[sl, 0]).start()
            remote(M1R, sl, dev_left, cbuf.at[sl, :, FAR, pl.ds(half, half)], m1.at[sl, 1]).start()

        def pass_sums(i, sl):
            wait(M1L, sl, dev_right, m1.at[sl, 0])
            wait(M1R, sl, dev_left, m1.at[sl, 1])
            for g in range(GROUP):
                cbuf[sl, g, RIGHT, 0:half] = cbuf[sl, g, RIGHT, 0:half] + m1[sl, 0, g]
                cbuf[sl, g, LEFT, half:own] = cbuf[sl, g, LEFT, half:own] + m1[sl, 1, g]
            remote(M2L, sl, dev_right, cbuf.at[sl, :, RIGHT], m2.at[sl, 0]).start()
            remote(M2R, sl, dev_left, cbuf.at[sl, :, LEFT], m2.at[sl, 1]).start()

        def finish_sums(i, sl):
            wait(M2L, sl, dev_right, m2.at[sl, 0])
            wait(M2R, sl, dev_left, m2.at[sl, 1])
            bias = b1[lax.div(i, groups)]
            for g in range(GROUP):
                h = (cbuf[sl, g, OWN] + m2[sl, 0, g]) + m2[sl, 1, g] + bias
                gall[sl, g, MINE, OWN] = gelu(h).astype(BF16)
            block = gall.at[sl, :, MINE, OWN]
            remote(GL, sl, dev_right, block, gall.at[sl, :, MINE, LEFT]).start()
            remote(GR, sl, dev_left, block, gall.at[sl, :, MINE, RIGHT]).start()
            remote(GP, sl, dev_pair, block, gall.at[sl, :, OTHER, OWN]).start()

        def forward(i, sl):
            wait(GL, sl, dev_right, gall.at[sl, :, MINE, LEFT])
            wait(GR, sl, dev_left, gall.at[sl, :, MINE, RIGHT])
            wait(GP, sl, dev_pair, gall.at[sl, :, OTHER, OWN])
            a, b = pl.ds(0, half), pl.ds(half, half)
            remote(FL, sl, dev_right, gall.at[sl, :, MINE, LEFT, a], gall.at[sl, :, MINE, FAR, a]).start()
            remote(FR, sl, dev_left, gall.at[sl, :, MINE, RIGHT, b], gall.at[sl, :, MINE, FAR, b]).start()

        def forward_far(i, sl):
            wait(FL, sl, dev_right, gall.at[sl, :, MINE, FAR, pl.ds(0, half)])
            wait(FR, sl, dev_left, gall.at[sl, :, MINE, FAR, pl.ds(half, half)])
            rest = pl.ds(RIGHT, chips - 1)
            remote(PX, sl, dev_pair, gall.at[sl, :, MINE, rest], gall.at[sl, :, OTHER, rest]).start()

        def complete(i, sl):
            wait(PX, sl, dev_pair, gall.at[sl, :, OTHER, pl.ds(RIGHT, chips - 1)])

        if point == 0:
            stage(s, 1, send_pair)
            stage(s, 3, pass_sums)
            stage(s, 4, finish_sums)
            stage(s, 7, complete)
        else:
            stage(s, 1, chip_sum)
            stage(s, 5, forward)
            stage(s, 6, forward_far)

    def unit(s, j, do_a, do_b, do_c, do_h):
        v_cur, v_next = (v0, v1) if (j + LAG) % 2 == 0 else (v1, v0)
        qa = s * GROUP + j - LAG
        qb, qc = qa - 1, qa + 1
        if do_a:
            la = lax.div(qa, batch)
        if do_b:
            lb = lax.div(jnp.maximum(qb, 0), batch)
            ib = jnp.where(qb < 0, batch, lax.rem(jnp.maximum(qb, 0), batch))
        if do_c:
            lc = jnp.minimum(lax.div(qc, batch), layers - 1)
            ic = jnp.where(qc >= items * GROUP, batch, lax.rem(qc, batch))
            gc = gall[lax.rem(lax.div(qc, GROUP), SLOTS), lax.rem(qc, GROUP)].reshape(2 * chips * own, chans)
            tb[...] = (dot(w2[lc], gc) + b2[lc]).astype(BF16)
        if do_h:
            lh = lax.div(s, groups)
            ih = lax.rem(s, groups) * GROUP + j
        blocks = wide // WIDTH
        share = rows // blocks
        acc = None
        for k in range(blocks):
            cols = slice(k * WIDTH, (k + 1) * WIDTH)
            if do_b:
                part = dot(act[:, cols], wc2[lb, cols, :])
                acc = part if acc is None else acc + part
            if do_a:
                act[:, cols] = gelu_of_half(dot(v_cur[...], wc1[la, :, cols]) + 0.5 * bc1[pl.ds(la, 1), cols]).astype(BF16)
            for r in range(k * share, (k + 1) * share, STRIP):
                strip = slice(r, r + STRIP)
                if do_c:
                    x1 = xb[ic, strip] + tb[strip]
                if do_h:
                    xh = xb[ih, strip]
                if do_c:
                    xb[ic, strip] = x1
                    v_next[strip] = norm(x1, ln[lc, 2:3], ln[lc, 3:4])
                if do_h:
                    ub[strip] = norm(xh, ln[lh, 0:1], ln[lh, 1:2])
        if do_b:
            xb[ib] = (xb[ib].astype(F32) + (acc + bc2[pl.ds(lb, 1), :])).astype(BF16)
        if do_h:
            hpart[lax.rem(s, HELD), j] = dot(w1[lh], ub[...]).reshape(2, chips, own, chans)

    def finished(s, j):
        before = items - groups
        i = s + (j - LAG) // GROUP

        @pl.when((i - 1 >= before) & (i - 1 < last))
        def _():
            store_z(i - 1 - before).start()

        @pl.when((i >= last) & (i < items))
        def _():
            store_z(i - before).start()

    def step(s, carry):
        @pl.when(s < groups)
        def _():
            load_x(s).wait()

        @pl.when(s == 1)
        def _():
            for c in mixing[1:]:
                c.wait()
            place_rest()

        @pl.when(s == 3)
        def _():
            for c in weight_copies():
                c.wait()

            def scale(r, carry):
                at = pl.ds(pl.multiple_of(r * 64, 64), 64)
                for l in range(layers):
                    wc1[l, at] = wc1[l, at] * jnp.asarray(0.5, BF16)
                return carry

            lax.fori_loop(0, chans // 64, scale, 0)

        for j in range(GROUP):
            exchange(s, j)

            n = s * GROUP + j

            @pl.when(n < LAG)
            def _():
                unit(s, j, False, False, False, True)

            @pl.when((n >= LAG) & (s < items))
            def _():
                unit(s, j, True, True, True, True)

            @pl.when((s >= items) & (n < stop))
            def _():
                unit(s, j, True, True, True, False)

            only_c = (n > stop) & (n < items * GROUP + LAG - 1)
            if (j + LAG) % GROUP == 0:
                @pl.when(n == stop)
                def _():
                    unit(s, j, False, True, True, False)
            else:
                only_c = only_c | (n == LAG - 1)

            @pl.when(only_c)
            def _():
                unit(s, j, False, False, True, False)

            if (j + LAG) % GROUP == 0:
                finished(s, j)

        return carry

    lax.fori_loop(0, items + LAG // GROUP, step, 0)

    def drain(g, carry):
        store_z(g).wait()
        return carry

    lax.fori_loop(0, groups, drain, 0)


def last_kernel(x_hbm, wc1_hbm, bc1, wc2_hbm, bc2, ln, z_hbm, xb, wc1, wc2, act, v0, v1, xsem, wsem, zsem):
    batch, rows, chans = x_hbm.shape
    layer = wc1_hbm.shape[0] - 1
    wide = wc1.shape[1]
    groups = batch // GROUP
    first = groups - LEFT_OVER
    pace = pl.cdiv(first, LEFT_OVER)

    def load(g):
        at = pl.ds(g * GROUP, GROUP)
        return pltpu.make_async_copy(x_hbm.at[at], xb.at[at], xsem.at[g])

    def store(g):
        at = pl.ds(g * GROUP, GROUP)
        return pltpu.make_async_copy(xb.at[at], z_hbm.at[at], zsem.at[g])

    weights = (pltpu.make_async_copy(wc1_hbm.at[layer], wc1, wsem.at[0]),
               pltpu.make_async_copy(wc2_hbm.at[layer], wc2, wsem.at[1]))
    load(first).start()
    for c in weights:
        c.start()
    for g in range(first + 1, groups):
        load(g).start()

    def prepare(v, i, strip):
        v[strip] = norm(xb[i, strip], ln[layer, 2:3], ln[layer, 3:4])

    def unit(i, v_cur, v_next, do_a):
        blocks = wide // WIDTH
        share = rows // blocks
        acc = None
        before = jnp.maximum(i - 1, first * GROUP)
        after = jnp.minimum(i + 1, batch - 1)
        for k in range(blocks):
            cols = slice(k * WIDTH, (k + 1) * WIDTH)
            part = dot(act[:, cols], wc2[cols])
            acc = part if acc is None else acc + part
            if do_a:
                pre = dot(v_cur[...], wc1[:, cols]) + 0.5 * bc1[layer:layer + 1, cols]
                act[:, cols] = gelu_of_half(pre).astype(BF16)
                for r in range(k * share, (k + 1) * share, STRIP):
                    prepare(v_next, after, slice(r, r + STRIP))
        z = (xb[before].astype(F32) + (acc + bc2[layer:layer + 1])).astype(BF16)
        return before, z

    load(first).wait()
    for r in range(0, rows, STRIP):
        prepare(v0, first * GROUP, slice(r, r + STRIP))
    for c in weights:
        c.wait()

    def scale(r, carry):
        at = pl.ds(pl.multiple_of(r * 64, 64), 64)
        wc1[at] = wc1[at] * jnp.asarray(0.5, BF16)
        return carry

    lax.fori_loop(0, chans // 64, scale, 0)
    for g in range(first):
        load(g).start()

    def pair(p, carry):
        g = first + p

        @pl.when(g + 1 < groups)
        def _():
            load(jnp.minimum(g + 1, groups - 1)).wait()

        before, z = unit(g * GROUP, v0, v1, True)

        @pl.when(p > 0)
        def _():
            xb[before] = z
            store(jnp.maximum(g - 1, first)).start()

        before, z = unit(g * GROUP + 1, v1, v0, True)
        xb[before] = z
        for n in range(pace):
            other = p * pace + n

            @pl.when(other < first)
            def _():
                load(jnp.minimum(other, first - 1)).wait()
                store(jnp.minimum(other, first - 1)).start()

        return carry

    lax.fori_loop(0, LEFT_OVER, pair, 0)
    before, z = unit(batch, v0, v1, False)
    xb[before] = z
    store(groups - 1).start()

    def drain(g, carry):
        store(g).wait()
        return carry

    lax.fori_loop(0, groups, drain, 0)


def solution(mesh):
    size = mesh.shape["seq"]
    chips = size // 2

    def local_layers(x, w_tok1, b_tok1, w_tok2, b_tok2, w_ch1, b_ch1, w_ch2, b_ch2, ln_params):
        layers = w_tok1.shape[0]
        batch, rows, chans = x.shape
        hid, wide = w_tok1.shape[2], w_ch1.shape[2]
        own = hid // size
        groups = batch // GROUP
        vmem = pl.BlockSpec(memory_space=pltpu.VMEM)
        hbm = pl.BlockSpec(memory_space=pl.ANY)
        tile = pltpu.VMEM((rows, chans), BF16)
        most = pl.pallas_call(
            functools.partial(kernel, chips),
            out_shape=jax.ShapeDtypeStruct(x.shape, BF16),
            in_specs=[hbm, hbm, vmem, hbm, vmem, hbm, vmem, hbm, vmem, vmem],
            out_specs=hbm,
            scratch_shapes=[
                pltpu.VMEM((batch + 1, rows, chans), BF16),
                pltpu.VMEM(w_ch1.shape, BF16),
                pltpu.VMEM(w_ch2.shape, BF16),
                pltpu.VMEM((rows, wide), BF16),
                tile, tile, tile, tile,
                pltpu.VMEM((HELD, GROUP, 2, chips, own, chans), F32),
                pltpu.VMEM((SLOTS, GROUP, chips, own, chans), F32),
                pltpu.VMEM((SLOTS, GROUP, chips, own, chans), F32),
                pltpu.VMEM((SLOTS, 2, GROUP, own // 2, chans), F32),
                pltpu.VMEM((SLOTS, 2, GROUP, own, chans), F32),
                pltpu.VMEM((SLOTS, GROUP, 2, chips, own, chans), BF16),
                pltpu.VMEM((layers, rows, hid), BF16),
                pltpu.VMEM((layers, hid, rows), BF16),
                pltpu.VMEM((layers, hid, rows), BF16),
                pltpu.VMEM((layers, rows, hid), BF16),
                pltpu.VMEM((layers, own, 1), F32),
                pltpu.VMEM((layers, rows, 1), F32),
                pltpu.SemaphoreType.DMA((groups,)),
                pltpu.SemaphoreType.DMA((5,)),
                pltpu.SemaphoreType.DMA((groups,)),
                pltpu.SemaphoreType.DMA((KINDS, SLOTS)),
                pltpu.SemaphoreType.DMA((KINDS, SLOTS)),
            ],
            compiler_params=pltpu.CompilerParams(
                collective_id=0, has_side_effects=True, vmem_limit_bytes=67043328),
        )(x, w_tok1, b_tok1, w_tok2, b_tok2, w_ch1, b_ch1, w_ch2, b_ch2, ln_params)
        return pl.pallas_call(
            last_kernel,
            out_shape=jax.ShapeDtypeStruct(x.shape, BF16),
            in_specs=[hbm, hbm, vmem, hbm, vmem, vmem],
            out_specs=hbm,
            scratch_shapes=[
                pltpu.VMEM(x.shape, BF16),
                pltpu.VMEM(w_ch1.shape[1:], BF16),
                pltpu.VMEM(w_ch2.shape[1:], BF16),
                pltpu.VMEM((rows, wide), BF16),
                tile, tile,
                pltpu.SemaphoreType.DMA((groups,)),
                pltpu.SemaphoreType.DMA((2,)),
                pltpu.SemaphoreType.DMA((groups,)),
            ],
            compiler_params=pltpu.CompilerParams(vmem_limit_bytes=67043328),
        )(most, w_ch1, b_ch1, w_ch2, b_ch2, ln_params)

    act = P("data", "seq", None)
    rep = P()
    return jax.shard_map(local_layers, mesh=mesh, in_specs=(act,) + (rep,) * 9, out_specs=act, check_vma=False)
```

time: 279 us -> 257 us (0.921)
  local copies, waits for them, and re-layouts: 23 us -> 0 us
    pallas_call x0 -> x1, Pallas kernels: none -> 18.2 us  [local_layers(): pl.pallas_call(last_kernel, out_shape=jax.ShapeDtypeStruct(x.shape, BF16)...]
    unnamed x3 -> x0, local copies, waits for them, and re-layouts: 15.8 us -> none
    pallas_call x1, Pallas kernels: 255 us -> 239 us  [local_layers(): pl.pallas_call(functools.partial(kernel, chips), out_shape=jax.ShapeDtype...]
    broadcast_in_dim x5 -> x0, local copies, waits for them, and re-layouts: 4.45 us -> none  [the longest x2 1.73 us: local_layers(): b2 = lax.dynamic_slice_in_dim(b_tok2, me * rows, rows, 1)[:, :, None]]
where the time goes in v3:
time: 257 us
  Pallas kernels  257 us (100%)
    pallas_call x1, Pallas kernels, local_layers(): pl.pallas_call(functools.partial(kernel, chips), out_shape=jax.ShapeDtype...  239 us
    pallas_call x1, Pallas kernels, local_layers(): pl.pallas_call(last_kernel, out_shape=jax.ShapeDtypeStruct(x.shape, BF16)...  18.2 us

profile of v3, /device:TPU:112, one launch (start us, length us, event | category | flops | bytes accessed | tf_op | source)
XLA Modules:
  0.0 257.2 jit_solution(16036077572935561247)
XLA Ops:
  0.0 238.9 %shard_map.100.x_hbm = bf16[32,512,512]{2,1,0:T(8,128)(2,1)} custom-call(bf16[32,512,512]{2,1,0:T(8,128)(2,1)} %x_hbm.1, bf16[2,4096,256]{2,1,0:T(8,128)(2,1)} %w1_hbm.1, f32[2,256]{1,0:T(2,128)} %b1_row.1, bf16[2,256,4096]{2,1,0:T(8,128)(2,1)} %w2_hbm.1, f32[2,4096]{1,0:T(2,128)} %b2_row.1, bf16[2,512,2048]{2,1,0:T(8,128)(2,1)} %wc1_hbm.3, f32[2,2048]{1,0:T(2,128)} %bc1.3, ...), custom_call_target="tpu_custom_call" | custom-call | tf_op jit(solution)/shard_map/pallas_call | solution.py:437
  238.9 18.2 %shard_map.101 = bf16[32,512,512]{2,1,0:T(8,128)(2,1)} custom-call(bf16[32,512,512]{2,1,0:T(8,128)(2,1)} %shard_map.100.x_hbm, bf16[2,512,2048]{2,1,0:T(8,128)(2,1)} %wc1_hbm.3, f32[2,2048]{1,0:T(2,128)} %bc1.3, bf16[2,2048,512]{2,1,0:T(8,128)(2,1)} %wc2_hbm.3, f32[2,512]{1,0:T(2,128)} %bc2.3, f32[2,4,512]{2,1,0:T(4,128)} %ln.3), custom_call_target="tpu_custom_call" | custom-call | tf_op jit(solution)/shard_map/pallas_call | solution.py:469

commit v4 on v3

--- a/solution.py
+++ b/solution.py
@@ -214,7 +214,6 @@
             lc = jnp.minimum(lax.div(qc, batch), layers - 1)
             ic = jnp.where(qc >= items * GROUP, batch, lax.rem(qc, batch))
             gc = gall[lax.rem(lax.div(qc, GROUP), SLOTS), lax.rem(qc, GROUP)].reshape(2 * chips * own, chans)
-            tb[...] = (dot(w2[lc], gc) + b2[lc]).astype(BF16)
         if do_h:
             lh = lax.div(s, groups)
             ih = lax.rem(s, groups) * GROUP + j
@@ -223,6 +222,9 @@
         acc = None
         for k in range(blocks):
             cols = slice(k * WIDTH, (k + 1) * WIDTH)
+            if do_c and k % (blocks // 2) == 0:
+                part_rows = slice(k * share, (k + blocks // 2) * share)
+                tb[part_rows] = (dot(w2[lc, part_rows], gc) + b2[lc, part_rows]).astype(BF16)
             if do_b:
                 part = dot(act[:, cols], wc2[lb, cols, :])
                 acc = part if acc is None else acc + part

time: 257 us -> 256 us (level)
  no operation moved by 1% of the time
where the time goes in v4:
time: 256 us; the launch traced here: 255 us
  Pallas kernels  255 us (100%)
    pallas_call x1, Pallas kernels, local_layers(): pl.pallas_call(functools.partial(kernel, chips), out_shape=jax.ShapeDtype...  237 us
    pallas_call x1, Pallas kernels, local_layers(): pl.pallas_call(last_kernel, out_shape=jax.ShapeDtypeStruct(x.shape, BF16)...  18.2 us

profile of v4, /device:TPU:112, one launch (start us, length us, event | category | flops | bytes accessed | tf_op | source)
XLA Modules:
  0.0 255.4 jit_solution(3530710094707894854)
XLA Ops:
  0.0 237.1 %shard_map.100.x_hbm = bf16[32,512,512]{2,1,0:T(8,128)(2,1)} custom-call(bf16[32,512,512]{2,1,0:T(8,128)(2,1)} %x_hbm.1, bf16[2,4096,256]{2,1,0:T(8,128)(2,1)} %w1_hbm.1, f32[2,256]{1,0:T(2,128)} %b1_row.1, bf16[2,256,4096]{2,1,0:T(8,128)(2,1)} %w2_hbm.1, f32[2,4096]{1,0:T(2,128)} %b2_row.1, bf16[2,512,2048]{2,1,0:T(8,128)(2,1)} %wc1_hbm.3, f32[2,2048]{1,0:T(2,128)} %bc1.3, ...), custom_call_target="tpu_custom_call" | custom-call | tf_op jit(solution)/shard_map/pallas_call | solution.py:439
  237.1 18.2 %shard_map.101 = bf16[32,512,512]{2,1,0:T(8,128)(2,1)} custom-call(bf16[32,512,512]{2,1,0:T(8,128)(2,1)} %shard_map.100.x_hbm, bf16[2,512,2048]{2,1,0:T(8,128)(2,1)} %wc1_hbm.3, f32[2,2048]{1,0:T(2,128)} %bc1.3, bf16[2,2048,512]{2,1,0:T(8,128)(2,1)} %wc2_hbm.3, f32[2,512]{1,0:T(2,128)} %bc2.3, f32[2,4,512]{2,1,0:T(4,128)} %ln.3), custom_call_target="tpu_custom_call" | custom-call | tf_op jit(solution)/shard_map/pallas_call | solution.py:471
